TPU v7x, 32 devices: a whole 2x2x4 slice. The times are simulated.
32 devices in a mesh: parts: 1, var: 8 (over z, core), patch: 4 (over y, x).
Axes of the slice: x: 2, y: 2, z: 4, core: 2. Of those that a mesh axis runs over, the one named last changes fastest.
Arguments:
- tokens: bfloat16 [256, 24, 768], P('patch', ('parts', 'var')), may hold values from -6 to 6
- patch_mask: int32 [256, 24], P('patch', ('parts', 'var')), may hold values 0 or 1
- group_ids: int32 [24], P('parts'), may hold values from 0 to 7, never falling along the last dimension, each value on 1 to 6 neighbouring positions
- time_gain: float32 [768], replicated, may hold values from 0.1 to 1.9
- time_qkv: bfloat16 [768, 3, 768], P(None, None, 'patch'), may hold values from -0.21875 to 0.21875
- time_out: bfloat16 [768, 768], P('patch'), may hold values from -0.21875 to 0.21875
- space_gain: float32 [768], replicated, may hold values from 0.1 to 1.9
- space_qkv: bfloat16 [768, 3, 768], P(None, None, 'patch'), may hold values from -0.21875 to 0.21875
- space_out: bfloat16 [768, 768], P('patch'), may hold values from -0.21875 to 0.21875
Outputs:
- panel_out: bfloat16 [256, 24, 768], P('patch', ('parts', 'var'))
Inputs may be any that keep to these rules, and one draw needn't show every extreme that they name: group_ids never falls along the variates; each group is a run of 1 to 6 consecutive variates.
All inputs are finite; a program needn't handle non-finite values. No bound on the sum of `patch_mask` on one device may be relied on, other than what follows from the above.
Results may differ from a plain program's by a relative error of at most 0.017.
Values may be sent and summed in bfloat16 or wider, within the bound.
A program may use at most 64 MiB of HBM per device.

v0:
```python
import jax
import jax.numpy as jnp
from jax import lax
from jax.sharding import PartitionSpec as P

HD = 64


epsilon = 1e-06


def passed_along(block, axis, distance):
    devices = range(lax.axis_size(axis))
    route = [(i - distance, i) for i in devices if i - distance in devices]
    return lax.ppermute(block, axis, route)


def norm_rows(block_rows, gain):
    floats = block_rows.astype(jnp.float32)
    scaled = floats * lax.rsqrt(jnp.mean(floats * floats, axis=-1, keepdims=True) + epsilon)
    return (scaled * gain).astype(jnp.bfloat16)


def soft_weights(scores, allowed):
    masked = jnp.where(allowed, scores, -jnp.inf)
    highest = jnp.max(masked, axis=-1, keepdims=True)
    raised = jnp.exp(masked - highest)
    return (raised / jnp.sum(raised, axis=-1, keepdims=True)).astype(jnp.bfloat16)


def make_term(attended, out_weight):
    return jnp.einsum("pvk,kd->pvd", attended, out_weight, preferred_element_type=jnp.float32)


def time_attend(normed, labels, weight):
    patch_count, var_count = (normed.shape[0], normed.shape[1])
    head_width = weight.shape[2]
    head_count = head_width // HD
    projected = jnp.einsum(
        "pvd,dtk->pvtk", normed, weight, preferred_element_type=jnp.float32
    ).astype(jnp.bfloat16)
    queries = projected[:, :, 0].reshape(patch_count, var_count, head_count, HD)
    key_rows = projected[:, :, 1].reshape(patch_count, var_count, head_count, HD)
    value_rows = projected[:, :, 2].reshape(patch_count, var_count, head_count, HD)
    scores = jnp.einsum(
        "qvhe,kvhe->vhqk", queries, key_rows, preferred_element_type=jnp.float32
    ) * HD ** (-0.5)
    query_pos = jnp.arange(patch_count)[:, None]
    key_pos = jnp.arange(patch_count)[None, :]
    observed = (labels.T > 0.5)[:, None, None, :]
    allowed = (key_pos <= query_pos)[None, None] & (observed | (key_pos == query_pos)[None, None])
    weights = soft_weights(scores, allowed)
    attended = jnp.einsum(
        "vhqk,kvhe->qvhe", weights, value_rows, preferred_element_type=jnp.float32
    ).astype(jnp.bfloat16)
    return attended.reshape(patch_count, var_count, head_width)


def space_attend(normed, group_ids, weight):
    patch_count, var_count = (normed.shape[0], normed.shape[1])
    head_width = weight.shape[2]
    head_count = head_width // HD
    projected = jnp.einsum(
        "pvd,dtk->pvtk", normed, weight, preferred_element_type=jnp.float32
    ).astype(jnp.bfloat16)
    queries = projected[:, :, 0].reshape(patch_count, var_count, head_count, HD)
    paired = projected[:, :, 1:3].reshape(patch_count, var_count, 2 * head_width)
    lower_list = []
    upper_list = []
    moving = paired
    for repeat in range(2):
        moving = passed_along(moving, "var", 1)
        lower_list.insert(0, moving)
    moving = paired
    for repeat in range(2):
        moving = passed_along(moving, "var", -1)
        upper_list.append(moving)
    window = jnp.concatenate(lower_list + [paired] + upper_list, axis=1)
    window_count = window.shape[1]
    key_window = window[:, :, :head_width].reshape(patch_count, window_count, head_count, HD)
    value_window = window[:, :, head_width:].reshape(patch_count, window_count, head_count, HD)
    device_index = lax.axis_index("var")
    outside = jnp.full((2 * var_count,), -1, jnp.int32)
    padded_ids = jnp.concatenate([outside, group_ids, outside])
    key_ids = lax.dynamic_slice_in_dim(padded_ids, device_index * var_count, window_count)
    query_ids = lax.dynamic_slice_in_dim(group_ids, device_index * var_count, var_count)
    scores = jnp.einsum(
        "pqhe,pkhe->phqk", queries, key_window, preferred_element_type=jnp.float32
    ) * HD ** (-0.5)
    allowed = (query_ids[:, None] == key_ids[None, :])[None, None]
    weights = soft_weights(scores, allowed)
    attended = jnp.einsum(
        "phqk,pkhe->pqhe", weights, value_window, preferred_element_type=jnp.float32
    ).astype(jnp.bfloat16)
    return attended.reshape(patch_count, var_count, head_width)


def on_device(
    tokens, patch_mask, group_ids, time_gain, time_qkv, time_out, space_gain, space_qkv, space_out
):
    mark_rows = patch_mask.astype(jnp.bfloat16)
    own_normed = norm_rows(tokens, time_gain)
    gathered, labels = (
        lax.all_gather(own_normed, "patch", axis=0, tiled=True),
        lax.all_gather(mark_rows, "patch", axis=0, tiled=True),
    )
    attended = time_attend(gathered, labels, time_qkv)
    summed = lax.psum_scatter(
        make_term(attended, time_out).astype(jnp.bfloat16), "patch", scatter_dimension=0, tiled=True
    ).astype(jnp.float32)
    residual = (tokens.astype(jnp.float32) + summed).astype(jnp.bfloat16)
    space_normed = lax.all_gather(norm_rows(residual, space_gain), "patch", axis=0, tiled=True)
    space_result = space_attend(space_normed, group_ids, space_qkv)
    space_summed = lax.psum_scatter(
        make_term(space_result, space_out).astype(jnp.bfloat16),
        "patch",
        scatter_dimension=0,
        tiled=True,
    ).astype(jnp.float32)
    return (residual.astype(jnp.float32) + space_summed).astype(jnp.bfloat16)


def solution(mesh):
    in_specs = (
        P("patch", ("parts", "var"), None),
        P("patch", ("parts", "var")),
        P("parts"),
        P(),
        P(None, None, "patch"),
        P("patch", None),
        P(),
        P(None, None, "patch"),
        P("patch", None),
    )
    out_specs = P("patch", ("parts", "var"), None)
    return jax.shard_map(
        on_device, mesh=mesh, in_specs=in_specs, out_specs=out_specs, check_vma=False
    )
```

profile of v0, /device:TPU:0, one launch (start us, length us, event | category | flops | bytes accessed | tf_op | source)
XLA Modules:
  0.0 196.2 jit_solution(7199102504552056548)
XLA Ops:
  6.5 0.0 copy-start
  6.5 0.0 all-gather.4.cloned.1.call-start
  6.5 1.2 fusion.14
  7.7 1.8 fusion.16
  9.5 0.0 all-gather.4.cloned.1.call-update
  9.6 0.0 reduce-scatter.3.cloned.1.call-start
  9.6 0.7 convert_bitcast_fusion
  10.3 9.6 %all-gather = bf16[4,64,3]{1,2,0:T(4,128)(2,1)S(1)} all-gather(bf16[1,64,3]{1,2,0:T(4,128)(2,1)S(1)} %convert_bitcast_fusion), channel_id=1, replica_groups=mesh['parts'=1,'var'=8,'patch'=4] {'patch'}, dimensions={0}, use_global_device_ids=true | all-gather | bytes 1920 | tf_op jit(solution)/shard_map/all_gather | solution.py:105
  19.9 0.1 reshape.108
  20.0 0.2 or_and_fusion
  20.2 19.8 %all-gather.4.cloned.1.call-done = bf16[256,3,768]{2,0,1:T(8,128)(2,1)} async-done(((bf16[64,3,768]{2,0,1:T(8,128)(2,1)}), bf16[256,3,768]{2,0,1:T(8,128)(2,1)}) %all-gather.4.cloned.1.call-update) | async-done | bytes 1179664 | tf_op jit(solution)/shard_map/all_gather | solution.py:104
  40.0 0.0 copy-done
  40.0 2.2 %convolution_convert_fusion.3 = bf16[256,3,3,192]{0,3,2,1:T(8,128)(2,1)S(1)} fusion(bf16[256,3,768]{2,0,1:T(8,128)(2,1)} %all-gather.4.cloned.1.call-done, bf16[768,3,192]{0,2,1:T(8,128)(2,1)S(1)} %copy-done), kind=kOutput, calls=%fused_computation.13 | convolution fusion | flops 679919616 | bytes 2949120 | tf_op jit(solution)/shard_map/pvd,dtk->pvtk/dot_general | solution.py:39
  42.2 0.1 fusion.29
  42.3 2.4 %fusion.30 = (f32[3,3,256]{2,1,0:T(4,128)S(1)}, f32[3,3,256,256]{2,3,1,0:T(8,128)}) fusion(pred[3,256,256]{1,2,0:T(8,128)(4,1)S(1)} %or_and_fusion, bf16[256,3,3,64]{0,3,2,1:T(8,128)(2,1)S(1)} %bitcast.57, bf16[256,3,3,64]{0,3,2,1:T(8,128)(2,1)S(1)} %bitcast.56), kind=kOutput, calls=%fused_computation.60 | convolution fusion | flops 77857024 | bytes 3154944 | tf_op jit(solution)/shard_map/sub | solution.py:27
  44.6 2.0 %convolution_convert_fusion.5 = bf16[3,3,64,256]{3,2,1,0:T(8,128)(2,1)S(1)} fusion(bf16[256,3,3,64]{0,3,2,1:T(8,128)(2,1)S(1)} %bitcast.55, f32[3,3,256,256]{2,3,1,0:T(8,128)} %get-tuple-element.11, f32[3,3,256]{2,1,0:T(4,128)S(1)} %get-tuple-element.10), kind=kOutput, calls=%fused_computation.16 | convolution fusion | flops 76824576 | bytes 2958336 | tf_op jit(solution)/shard_map/vhqk,kvhe->qvhe/dot_general | solution.py:53
  46.7 0.0 copy-start.1
  46.7 0.0 copy-start.5
  46.7 0.0 copy-done.3
  46.7 1.5 convolution_convert_fusion.1
  48.3 0.0 reduce-scatter.3.cloned.1.call-update
  48.3 0.0 all-gather.6.cloned.1.call-start
  48.4 28.8 %reduce-scatter.3.cloned.1.call-done = bf16[64,3,768]{2,0,1:T(8,128)(2,1)} async-done(((bf16[256,3,768]{2,0,1:T(8,128)(2,1)}), bf16[64,3,768]{2,0,1:T(8,128)(2,1)}) %reduce-scatter.3.cloned.1.call-update) | async-done | bytes 294928 | tf_op jit(solution)/shard_map/reduce_scatter | solution.py:108
  77.2 0.0 copy-done.1
  77.2 1.1 fusion.18
  78.3 0.0 copy-done.5
  78.3 1.8 fusion.20
  80.1 0.0 all-gather.6.cloned.1.call-update
  80.1 0.0 copy-start.6
  80.2 0.0 reduce-scatter.5.cloned.1.call-start
  80.2 27.7 %all-gather.6.cloned.1.call-done = bf16[256,3,768]{2,0,1:T(8,128)(2,1)} async-done(((bf16[64,3,768]{2,0,1:T(8,128)(2,1)}), bf16[256,3,768]{2,0,1:T(8,128)(2,1)}) %all-gather.6.cloned.1.call-update) | async-done | bytes 1179664 | tf_op jit(solution)/shard_map/all_gather | solution.py:112
  107.9 2.4 %convolution_convert_fusion.2 = bf16[256,3,3,192]{0,3,2,1:T(8,128)(2,1)S(1)} fusion(bf16[256,3,768]{2,0,1:T(8,128)(2,1)} %all-gather.6.cloned.1.call-done, bf16[768,3,192]{0,2,1:T(8,128)(2,1)} %param.16), kind=kOutput, calls=%fused_computation.12 | convolution fusion | flops 679919616 | bytes 2949120 | tf_op jit(solution)/shard_map/pvd,dtk->pvtk/dot_general | solution.py:63
  110.3 2.4 %collective-permute-start = (bf16[256,3,384]{0,2,1:T(8,128)(2,1)S(1)}, bf16[256,3,384]{0,2,1:T(8,128)(2,1)}, u32[]{:S(2)}, u32[]{:S(2)}) collective-permute-start(bf16[256,3,384]{0,2,1:T(8,128)(2,1)S(1)} %bitcast.50), channel_id=1, source_target_pairs={{0,4},{4,8},{8,12},{12,16},{16,20},{20,24},{24,28},{1,5},{5,9},{9,... | collective-permute-start | bytes 1769480 | tf_op jit(solution)/shard_map/ppermute | solution.py:15
  112.8 1.3 collective-permute-start.2
  114.0 0.0 collective-permute-done
  114.0 9.4 %collective-permute-start.1 = (bf16[256,3,384]{0,2,1:T(8,128)(2,1)}, bf16[256,3,384]{0,2,1:T(8,128)(2,1)}, u32[]{:S(2)}, u32[]{:S(2)}) collective-permute-start(bf16[256,3,384]{0,2,1:T(8,128)(2,1)} %collective-permute-done), channel_id=1, source_target_pairs={{0,4},{4,8},{8,12},{12,16},{16,20},{20,24},{24,28},{1,5},{5,9},{9,... | collective-permute-start | bytes 1769480 | tf_op jit(solution)/shard_map/ppermute | solution.py:15
  123.4 0.0 copy-done.6
  123.4 0.1 dynamic_slice.6
  123.5 0.1 pad_add_fusion
  123.6 0.1 dynamic_slice.7
  123.6 0.0 collective-permute-done.2
  123.6 1.3 collective-permute-start.3
  124.9 0.1 broadcast_compare_fusion
  125.0 0.6 copy.26
  125.6 0.0 collective-permute-done.1
  125.6 1.1 constant_dynamic-update-slice_fusion.4
  126.7 1.1 constant_dynamic-update-slice_fusion.3
  127.9 1.1 constant_dynamic-update-slice_fusion.1
  129.0 0.2 collective-permute-done.3
  129.1 1.1 constant_dynamic-update-slice_fusion
  130.3 1.4 fusion.28
  131.6 5.2 %copy.27 = bf16[256,15,3,64]{3,1,2,0:T(8,128)(2,1)} copy(bf16[256,15,3,64]{0,3,2,1:T(8,128)(2,1)} %bitcast.49) | data formatting | bytes 2949120 | tf_op jit(solution)/shard_map/reshape | solution.py:80
  136.9 3.9 %copy.28 = bf16[256,15,3,64]{3,1,2,0:T(8,128)(2,1)} copy(bf16[256,15,3,64]{0,3,2,1:T(8,128)(2,1)S(1)} %bitcast.48) | data formatting | bytes 2949120 | tf_op jit(solution)/shard_map/reshape | solution.py:81
  140.8 5.0 %fusion.31 = (f32[256,3,3]{2,1,0:T(4,128)S(1)}, f32[256,3,3,15]{3,2,1,0:T(4,128)}) fusion(bf16[256,3,3,64]{3,1,2,0:T(4,128)(2,1)S(1)} %copy.26, bf16[256,15,3,64]{3,1,2,0:T(8,128)(2,1)} %copy.27, pred[3,15]{1,0:T(4,128)(4,1)S(1)} %broadcast_compare_fusion), kind=kOutput, calls=%fused_computation.61 | convolution fusion | flops 4561934 | bytes 1916973 | tf_op jit(solution)/shard_map/sub | solution.py:27
  145.8 0.0 copy-start.4
  145.8 3.6 %fusion.5 = bf16[256,3,3,64]{3,1,2,0:T(4,128)(2,1)S(1)} fusion(bf16[256,15,3,64]{3,1,2,0:T(8,128)(2,1)} %copy.28, f32[256,3,3,15]{3,2,1,0:T(4,128)} %get-tuple-element.13, f32[256,3,3]{2,1,0:T(4,128)S(1)} %get-tuple-element.12), kind=kOutput, calls=%fused_computation.15 | convolution fusion | flops 4640256 | bytes 1916928 | tf_op jit(solution)/shard_map/phqk,pkhe->pqhe/dot_general | solution.py:92
  149.4 0.0 copy-start.2
  149.4 0.5 copy.29
  150.0 0.0 copy-done.4
  150.0 1.5 convolution_convert_fusion
  151.5 0.0 reduce-scatter.5.cloned.1.call-update
  151.6 36.3 %reduce-scatter.5.cloned.1.call-done = bf16[64,3,768]{2,0,1:T(8,128)(2,1)} async-done(((bf16[256,3,768]{2,0,1:T(8,128)(2,1)}), bf16[64,3,768]{2,0,1:T(8,128)(2,1)}) %reduce-scatter.5.cloned.1.call-update) | async-done | bytes 294928 | tf_op jit(solution)/shard_map/reduce_scatter | solution.py:114
  187.8 0.0 copy-done.2
  187.8 1.8 fusion.21
  (9 shorter events, 0.2 us)
Async XLA Ops:
  6.5 33.5 %copy-start = (bf16[768,3,192]{0,2,1:T(8,128)(2,1)S(1)}, bf16[768,3,192]{0,2,1:T(8,128)(2,1)}, u32[]{:S(2)}) copy-start(bf16[768,3,192]{0,2,1:T(8,128)(2,1)} %param.13) | copy-start | bytes 2654212
  6.5 33.5 %all-gather.4.cloned.1.call-start = ((), (), s32[]{:S(2)}) async-start(), calls=%async_computation.2 | async-start | bytes 1474560 | tf_op jit(solution)/shard_map/all_gather | solution.py:104
  9.6 67.6 %reduce-scatter.3.cloned.1.call-start = ((), (), s32[]{:S(2)}) async-start(), calls=%async_computation.3 | async-start | bytes 1474560 | tf_op jit(solution)/shard_map/reduce_scatter | solution.py:108
  44.6 2.1 %copy-start.3 = (bf16[192,768]{1,0:T(8,128)(2,1)S(1)}, bf16[192,768]{1,0:T(8,128)(2,1)}, u32[]{:S(2)}) copy-start(bf16[192,768]{1,0:T(8,128)(2,1)} %param.14) | copy-start | bytes 884740
  46.7 30.5 %copy-start.1 = (bf16[64,3,768]{2,0,1:T(8,128)(2,1)S(1)}, bf16[64,3,768]{2,0,1:T(8,128)(2,1)}, u32[]{:S(2)}) copy-start(bf16[64,3,768]{2,0,1:T(8,128)(2,1)} %param.9) | copy-start | bytes 884740
  46.7 31.6 %copy-start.5 = (f32[768]{0:T(1024)S(1)}, f32[768]{0:T(1024)}, u32[]{:S(2)}) copy-start(f32[768]{0:T(1024)} %param.15) | copy-start | bytes 9220
  48.3 59.6 %all-gather.6.cloned.1.call-start = ((), (), s32[]{:S(2)}) async-start(), calls=%async_computation.4 | async-start | bytes 1474560 | tf_op jit(solution)/shard_map/all_gather | solution.py:112
  80.1 43.3 %copy-start.6 = (s32[24]{0:T(128)S(1)}, s32[24]{0:T(128)}, u32[]{:S(2)}) copy-start(s32[24]{0:T(128)} %param.11) | copy-start | bytes 292
  80.2 107.7 %reduce-scatter.5.cloned.1.call-start = ((), (), s32[]{:S(2)}) async-start(), calls=%async_computation.5 | async-start | bytes 1474560 | tf_op jit(solution)/shard_map/reduce_scatter | solution.py:114
  110.3 3.7 %collective-permute-start = (bf16[256,3,384]{0,2,1:T(8,128)(2,1)S(1)}, bf16[256,3,384]{0,2,1:T(8,128)(2,1)}, u32[]{:S(2)}, u32[]{:S(2)}) collective-permute-start(bf16[256,3,384]{0,2,1:T(8,128)(2,1)S(1)} %bitcast.50), channel_id=1, source_target_pairs={{0,4},{4,8},{8,12},{12,16},{16,20},{20,24},{24,28},{1,5},{5,9},{9,... | collective-permute-start | bytes 1769480 | tf_op jit(solution)/shard_map/ppermute | solution.py:15
  112.8 10.9 %collective-permute-start.2 = (bf16[256,3,384]{0,2,1:T(8,128)(2,1)S(1)}, bf16[256,3,384]{0,2,1:T(8,128)(2,1)}, u32[]{:S(2)}, u32[]{:S(2)}) collective-permute-start(bf16[256,3,384]{0,2,1:T(8,128)(2,1)S(1)} %bitcast.51), channel_id=1, source_target_pairs={{4,0},{8,4},{12,8},{16,12},{20,16},{24,20},{28,24},{5,1},{9,5},{13... | collective-permute-start | bytes 1769480 | tf_op jit(solution)/shard_map/ppermute | solution.py:15
  114.0 11.5 %collective-permute-start.1 = (bf16[256,3,384]{0,2,1:T(8,128)(2,1)}, bf16[256,3,384]{0,2,1:T(8,128)(2,1)}, u32[]{:S(2)}, u32[]{:S(2)}) collective-permute-start(bf16[256,3,384]{0,2,1:T(8,128)(2,1)} %collective-permute-done), channel_id=1, source_target_pairs={{0,4},{4,8},{8,12},{12,16},{16,20},{20,24},{24,28},{1,5},{5,9},{9,... | collective-permute-start | bytes 1769480 | tf_op jit(solution)/shard_map/ppermute | solution.py:15
  123.6 5.5 %collective-permute-start.3 = (bf16[256,3,384]{0,2,1:T(8,128)(2,1)}, bf16[256,3,384]{0,2,1:T(8,128)(2,1)}, u32[]{:S(2)}, u32[]{:S(2)}) collective-permute-start(bf16[256,3,384]{0,2,1:T(8,128)(2,1)} %collective-permute-done.2), channel_id=1, source_target_pairs={{4,0},{8,4},{12,8},{16,12},{20,16},{24,20},{28,24},{5,1},{9,5},{13... | collective-permute-start | bytes 1769480 | tf_op jit(solution)/shard_map/ppermute | solution.py:15
  145.8 4.2 %copy-start.4 = (bf16[192,768]{1,0:T(8,128)(2,1)S(1)}, bf16[192,768]{1,0:T(8,128)(2,1)}, u32[]{:S(2)}) copy-start(bf16[192,768]{1,0:T(8,128)(2,1)} %param.17) | copy-start | bytes 884740
  149.4 38.4 %copy-start.2 = (bf16[64,3,768]{2,0,1:T(8,128)(2,1)S(1)}, bf16[64,3,768]{2,0,1:T(8,128)(2,1)}, u32[]{:S(2)}) copy-start(bf16[64,3,768]{2,0,1:T(8,128)(2,1)} %reduce-scatter.3.cloned.1.call-done) | copy-start | bytes 884740
Sparse Core Ops, SparseCore 0:
  9.7 30.2 all-gather.3
  48.4 28.6 reduce-scatter.2
  80.3 27.5 all-gather.5
  151.7 36.1 reduce-scatter.4
where the time goes:
time: 197 us; the launch traced here: 196 us
  waiting for transfers between devices  113 us (57%)
  matrix products  20.7 us (11%)
  local copies, waits for them, and re-layouts  16.5 us (8%)
  starting transfers between devices  14.5 us (7%)
  between operations  13.3 us (7%)
  blocking collectives  9.56 us (5%)
  other arithmetic  8.81 us (4%)
    reduce_scatter x1, waiting for transfers between devices, on_device(): lax.psum_scatter(make_term(space_result, space_out).astype(jnp.bfloat16),...  36.3 us
    reduce_scatter x1, waiting for transfers between devices, on_device(): lax.psum_scatter(make_term(attended, time_out).astype(jnp.bfloat16), 'pat...  28.8 us
    all_gather x1, waiting for transfers between devices, on_device(): lax.all_gather(norm_rows(residual, space_gain), 'patch', axis=0, tiled=True)  27.7 us
    all_gather x1, waiting for transfers between devices, on_device(): lax.all_gather(own_normed, 'patch', axis=0, tiled=True)  19.8 us
    ppermute x4, starting transfers between devices, passed_along(): return lax.ppermute(block, axis, route)  14.3 us
    all_gather x1, blocking collectives, on_device(): lax.all_gather(mark_rows, 'patch', axis=0, tiled=True)  9.56 us
    sub x2, matrix products, soft_weights(): raised = jnp.exp(masked - highest)  7.41 us
    reshape x1, local copies, waits for them, and re-layouts, space_attend(): window[:, :, :head_width].reshape(patch_count, window_count, head_count, HD)  5.24 us
  transfers between devices with their start and end apart: 8, of which 5 were waited for; matrix products, arithmetic and copies ran while one was open for 3% of the time, Pallas kernels for 0%

commit v1 on v0

v1 whole, which is shorter than its diff:
```python
import functools

import jax
import jax.numpy as jnp
from jax import lax
from jax.experimental import pallas as pl
from jax.experimental.pallas import tpu as pltpu
from jax.sharding import PartitionSpec as P

HD = 64
REACH = 5
EPS = 1e-06
MESH = pl.DeviceIdType.MESH
F32 = jnp.float32
BF16 = jnp.bfloat16


def norm_rows(rows, gain):
    floats = rows.astype(F32)
    scaled = floats * lax.rsqrt(jnp.mean(floats * floats, axis=-1, keepdims=True) + EPS)
    return (scaled * gain).astype(BF16)


def dot(a, b):
    return jnp.dot(a, b, preferred_element_type=F32)


def kernel(
    n, nvar, tok, marks, gids, tgain, sgain, wt_in, wot_in, wqs_in, wos_in,
    out, gx, mk, wt, wot, wqs, wos, att, ratt, mid, sw, kvb, qb, prod, sc, pb,
    local_sem, tok_s, tok_r, mk_s, mk_r, w_s, w_r, att_s, att_r, win_s, win_r,
):
    me = lax.axis_index("patch")
    var = lax.axis_index("var")
    nv, pp, dm = tok.shape
    hw = wot_in.shape[0]
    heads = hw // HD
    sib = var + 1 - 2 * (var % 2)
    par = var + 2 - 4 * ((var // 2) % 2)
    quarter = var % 4
    sib_q = sib % 4
    par_q = par % 4
    nbrs = (1, -1, 2, -2)

    def exists(k):
        return (var + k >= 0) & (var + k < nvar)

    def peer(d):
        return (me + d) % n

    def source(d):
        return (me + n - d) % n

    barrier = pltpu.get_barrier_semaphore()
    count = n - 1 + 2
    for d in range(1, n):
        pl.semaphore_signal(barrier, inc=1, device_id={"patch": peer(d)}, device_id_type=MESH)
    for other in (sib, par):
        pl.semaphore_signal(barrier, inc=1, device_id={"var": other}, device_id_type=MESH)
    for k in nbrs:
        @pl.when(exists(k))
        def _():
            pl.semaphore_signal(barrier, inc=1, device_id={"var": var + k}, device_id_type=MESH)
        count = count + exists(k).astype(jnp.int32)
    pl.semaphore_wait(barrier, count)

    sends = []

    def remote(src, dst, ssem, rsem, **where):
        c = pltpu.make_async_remote_copy(
            src_ref=src, dst_ref=dst, send_sem=ssem, recv_sem=rsem, device_id=where, device_id_type=MESH
        )
        return c

    def launch(*a, **k):
        c = remote(*a, **k)
        c.start()
        sends.append(c)
        return c

    mine = pl.ds(pl.multiple_of(me * pp, pp), pp)
    tok_c, mk_c = [], []
    for d in range(1, n):
        mk_c.append(launch(marks, mk.at[me], mk_s.at[d], mk_r.at[d], patch=peer(d)))
    for d in (1, 3, 2) if n == 4 else range(1, n):
        tok_c.append(launch(tok, gx.at[:, mine, :], tok_s.at[d], tok_r.at[d], patch=peer(d)))

    arrays = ((wot_in, wot), (wqs_in, wqs), (wos_in, wos))

    def part(buf, shard, q):
        rows = buf.shape[1] // 4
        return buf.at[shard, pl.ds(pl.multiple_of(q * rows, rows), rows), :]

    first = {}
    for a, (src, dst) in enumerate(arrays):
        rows = src.shape[0] // 4
        for d in range(1, n):
            first[a, d] = launch(
                src.at[pl.ds(pl.multiple_of(quarter * rows, rows), rows), :], part(dst, me, quarter),
                w_s.at[0, a, d], w_r.at[0, a, d], patch=peer(d),
            )
    second, third, fourth = {}, {}, {}

    def forward(a):
        buf = arrays[a][1]
        for d in range(1, n):
            first[a, d].wait_recv()
            piece = part(buf, source(d), quarter)
            third[a, d] = launch(piece, piece, w_s.at[2, a, d], w_r.at[2, a, d], var=par)
            second[a, d] = launch(piece, piece, w_s.at[1, a, d], w_r.at[1, a, d], var=sib)

    def relay(a):
        buf = arrays[a][1]
        for d in range(1, n):
            third[a, d].wait_recv()
            piece = part(buf, source(d), par_q)
            fourth[a, d] = launch(piece, piece, w_s.at[3, a, d], w_r.at[3, a, d], var=sib)

    def arrived(a):
        for d in range(1, n):
            second[a, d].wait_recv()
            fourth[a, d].wait_recv()

    own = [
        pltpu.make_async_copy(wt_in, wt, local_sem.at[0]),
        pltpu.make_async_copy(wot_in, wot.at[me], local_sem.at[1]),
        pltpu.make_async_copy(wqs_in, wqs.at[me], local_sem.at[2]),
        pltpu.make_async_copy(wos_in, wos.at[me], local_sem.at[3]),
    ]
    for c in own:
        c.start()

    for k in nbrs:
        lo = {1: 9, -1: 3, 2: 12, -2: 1}[k]
        num = nv if abs(k) == 1 else nv - 1

        @pl.when(jnp.logical_not(exists(k)))
        def _():
            sw[lo:lo + num] = jnp.zeros((num, pp, dm), BF16)

    gx[:, mine, :] = tok[...]
    mk[me] = marks[...]
    own[0].wait()
    for c in mk_c:
        c.wait_recv()
    for c in tok_c:
        c.wait_recv()

    full = n * pp
    seen = mk[0]
    for s in range(1, n):
        seen = seen + mk[s]
    qi = lax.broadcasted_iota(jnp.int32, (full, full), 0)
    ki = lax.broadcasted_iota(jnp.int32, (full, full), 1)
    att_c = []
    for v in range(nv):
        normed = norm_rows(gx[v], tgain[...])
        proj = dot(normed, wt[...]).astype(BF16)
        allowed = ((ki < qi) & (seen[v:v + 1, :] > 0.5)) | (ki == qi)
        outs = []
        for h in range(heads):
            q = proj[:, h * HD:(h + 1) * HD]
            k = proj[:, hw + h * HD:hw + (h + 1) * HD]
            val = proj[:, 2 * hw + h * HD:2 * hw + (h + 1) * HD]
            s = lax.dot_general(q, k, (((1,), (1,)), ((), ())), preferred_element_type=F32) * HD ** (-0.5)
            s = jnp.where(allowed, s, -jnp.inf)
            e = jnp.exp(s - jnp.max(s, axis=-1, keepdims=True))
            w = (e / jnp.sum(e, axis=-1, keepdims=True)).astype(BF16)
            outs.append(dot(w, val).astype(BF16))
        att[v] = jnp.concatenate(outs, axis=1)
        for d in range(1, n):
            there = pl.ds(pl.multiple_of(peer(d) * pp, pp), pp)
            att_c.append(launch(att.at[v, there, :], ratt.at[me, v], att_s.at[v, d], att_r.at[v, d], patch=peer(d)))
        ratt[me, v] = att[v, mine, :]
        if v == 0:
            forward(0)
        if v == 1:
            forward(1)
    relay(0)
    own[1].wait()
    arrived(0)
    for c in att_c:
        c.wait_recv()

    rows = nv * pp
    mix = jnp.zeros((rows, dm), F32)
    for s in range(n):
        mix = mix + dot(ratt[s].reshape(rows, hw), wot[s]).astype(BF16).astype(F32)
    middle = (tok[...].reshape(rows, dm).astype(F32) + mix).astype(BF16)
    mid[...] = middle
    sw[6:6 + nv] = norm_rows(middle, sgain[...]).reshape(nv, pp, dm)

    def window(k, i):
        src = {1: (6, 9), -1: (6, 9), 2: (7, 9), -2: (6, 8)}[k]
        dst = {1: (3, 6), -1: (9, 12), 2: (1, 3), -2: (12, 14)}[k]
        return remote(sw.at[src[0]:src[1]], sw.at[dst[0]:dst[1]], win_s.at[i], win_r.at[i], var=var + k)

    for i, k in enumerate(nbrs):
        @pl.when(exists(k))
        def _():
            window(k, i).start()

    forward(2)
    relay(1)
    own[2].wait()
    arrived(1)
    for i, k in enumerate(nbrs):
        @pl.when(exists(-k))
        def _():
            window(k, i).wait_recv()

    nkey = 4 + 3 * nv
    pairs = [(u, u + 6 + t) for u in range(nv) for t in range(-REACH, REACH + 1)]
    sc[...] = jnp.zeros_like(sc)

    def scores_of(s, carry):
        qb[...] = dot(sw[6:6 + nv].reshape(rows, dm), wqs[s, :, 2 * hw:]).astype(BF16).reshape(nv, pp, hw)
        kvb[s] = dot(sw[1:1 + nkey].reshape(nkey * pp, dm), wqs[s, :, :2 * hw]).astype(BF16).reshape(nkey, pp, 2 * hw)
        for i, (u, j) in enumerate(pairs):
            prod[i * pp:(i + 1) * pp, :] = (
                qb[u].astype(F32) * kvb[s, j - 1, :, :hw].astype(F32)
            ).astype(BF16)
        lane = lax.broadcasted_iota(jnp.int32, (hw, 128), 0) // HD + heads * s
        col = lax.broadcasted_iota(jnp.int32, (hw, 128), 1)
        sc[...] += dot(prod[...], (lane == col).astype(F32).astype(BF16))
        return carry

    lax.fori_loop(0, n, scores_of, 0)

    total = gids.shape[0]
    local_n = total // nv
    base = (var % local_n) * nv
    for u in range(nv):
        mine_group = gids[base + u]
        slabs = []
        for t in range(-REACH, REACH + 1):
            w = base + u + t
            inside = (w >= 0) & (w < total)
            at = jnp.minimum(jnp.maximum(w, 0), total - 1)
            i = pairs.index((u, u + 6 + t))
            ok = inside & (gids[at] == mine_group)
            slabs.append(jnp.where(ok, sc[i * pp:(i + 1) * pp, :] * HD ** (-0.5), -jnp.inf))
        top = functools.reduce(jnp.maximum, slabs)
        es = [jnp.exp(x - top) for x in slabs]
        den = functools.reduce(lambda a, b: a + b, es)
        for t, e in enumerate(es):
            i = u * (2 * REACH + 1) + t
            pb[i * pp:(i + 1) * pp, :] = (e / den).astype(BF16)

    relay(2)
    own[3].wait()
    arrived(2)

    def mix_of(s, acc):
        lane = lax.broadcasted_iota(jnp.int32, (128, hw), 1) // HD + heads * s
        col = lax.broadcasted_iota(jnp.int32, (128, hw), 0)
        spread = (lane == col).astype(F32).astype(BF16)
        done = []
        for u in range(nv):
            total_u = jnp.zeros((pp, hw), F32)
            lo = u * (2 * REACH + 1)
            wide = dot(pb[lo * pp:(lo + 2 * REACH + 1) * pp, :], spread)
            for t in range(2 * REACH + 1):
                val = kvb[s, u + t, :, hw:].astype(F32)
                total_u = total_u + wide[t * pp:(t + 1) * pp] * val
            done.append(total_u.astype(BF16))
        res = dot(jnp.concatenate(done, axis=0), wos[s]).astype(BF16).astype(F32)
        return acc + res

    mix2 = lax.fori_loop(0, n, mix_of, jnp.zeros((rows, dm), F32))
    out[...] = (mid[...].astype(F32) + mix2).astype(BF16).reshape(nv, pp, dm)

    for c in sends:
        c.wait_send()
    for i, k in enumerate(nbrs):
        @pl.when(exists(k))
        def _():
            window(k, i).wait_send()


def on_device(n, nvar, tokens, patch_mask, group_ids, time_gain, time_qkv, time_out, space_gain, space_qkv, space_out):
    pp, nv, dm = tokens.shape
    hw = time_out.shape[0]
    me = lax.axis_index("patch")
    tok = jnp.transpose(tokens, (1, 0, 2))
    marks = lax.dynamic_update_slice(
        jnp.zeros((8, n * pp), F32), patch_mask.T.astype(F32), (0, me * pp)
    )
    wt = time_qkv.reshape(dm, 3 * hw)
    wqs = jnp.concatenate([space_qkv[:, 1], space_qkv[:, 2], space_qkv[:, 0]], axis=1)
    npair = nv * (2 * REACH + 1)
    vm = pl.BlockSpec(memory_space=pltpu.VMEM)
    anyv = pl.BlockSpec(memory_space=pl.ANY)
    dma = pltpu.SemaphoreType.DMA
    res = pl.pallas_call(
        functools.partial(kernel, n, nvar),
        out_shape=jax.ShapeDtypeStruct((nv, pp, dm), BF16),
        in_specs=[vm, vm, pl.BlockSpec(memory_space=pltpu.SMEM), vm, vm, anyv, anyv, anyv, anyv],
        out_specs=vm,
        scratch_shapes=[
            pltpu.VMEM((nv, n * pp, dm), BF16),
            pltpu.VMEM((n, 8, n * pp), F32),
            pltpu.VMEM((dm, 3 * hw), BF16),
            pltpu.VMEM((n, hw, dm), BF16),
            pltpu.VMEM((n, dm, 3 * hw), BF16),
            pltpu.VMEM((n, hw, dm), BF16),
            pltpu.VMEM((nv, n * pp, hw), BF16),
            pltpu.VMEM((n, nv, pp, hw), BF16),
            pltpu.VMEM((nv * pp, dm), BF16),
            pltpu.VMEM((5 * nv, pp, dm), BF16),
            pltpu.VMEM((n, 4 + 3 * nv, pp, 2 * hw), BF16),
            pltpu.VMEM((nv, pp, hw), BF16),
            pltpu.VMEM((npair * pp, hw), BF16),
            pltpu.VMEM((npair * pp, 128), F32),
            pltpu.VMEM((npair * pp, 128), BF16),
            dma((4,)), dma((n,)), dma((n,)), dma((n,)), dma((n,)),
            dma((4, 3, n)), dma((4, 3, n)), dma((nv, n)), dma((nv, n)), dma((4,)), dma((4,)),
        ],
        compiler_params=pltpu.CompilerParams(
            collective_id=0, has_side_effects=True, vmem_limit_bytes=52 * 2**20
        ),
    )(tok, marks, group_ids, time_gain[None], space_gain[None], wt, time_out, wqs, space_out)
    return jnp.transpose(res, (1, 0, 2))


def solution(mesh):
    in_specs = (
        P("patch", ("parts", "var"), None),
        P("patch", ("parts", "var")),
        P("parts"),
        P(),
        P(None, None, "patch"),
        P("patch", None),
        P(),
        P(None, None, "patch"),
        P("patch", None),
    )
    out_specs = P("patch", ("parts", "var"), None)
    return jax.shard_map(
        functools.partial(on_device, mesh.shape["patch"], mesh.shape["var"]),
        mesh=mesh, in_specs=in_specs, out_specs=out_specs, check_vma=False,
    )
```

time: 197 us -> 74.8 us (0.38)
  waiting for transfers between devices: 113 us -> 0 us
  Pallas kernels: 0 us -> 66.1 us
  matrix products: 20.7 us -> 0 us
  starting transfers between devices: 14.5 us -> 0 us
  between operations: 13.3 us -> 0.07 us
  local copies, waits for them, and re-layouts: 16.5 us -> 5.39 us
  blocking collectives: 9.56 us -> 0 us
  other arithmetic: 8.81 us -> 2.04 us
    pallas_call x0 -> x1, Pallas kernels: none -> 66.1 us  [on_device(): pl.pallas_call(functools.partial(kernel, n, nvar), out_shape=jax.ShapeDty...]
    reduce_scatter x2 -> x0, waiting for transfers between devices: 65.1 us -> none  [the longest x1 36.3 us: on_device(): lax.psum_scatter(make_term(space_result, space_out).astype(jnp.bfloat16),...]
    all_gather x2 -> x0, waiting for transfers between devices: 47.5 us -> none  [the longest x1 27.7 us: on_device(): lax.all_gather(norm_rows(residual, space_gain), 'patch', axis=0, tiled=True)]
    ppermute x4 -> x0, starting transfers between devices: 14.3 us -> none  [passed_along(): return lax.ppermute(block, axis, route)]
    dot_general x6 -> x0, matrix products: 13.3 us -> none  [the longest x1 3.59 us: space_attend(): jnp.einsum('phqk,pkhe->pqhe', weights, value_window, preferred_element_ty...]
    all_gather x1 -> x0, blocking collectives: 9.56 us -> none  [on_device(): lax.all_gather(mark_rows, 'patch', axis=0, tiled=True)]
    reshape x2 -> x1, local copies, waits for them, and re-layouts: 9.17 us -> 1.32 us  [on_device(): wt = time_qkv.reshape(dm, 3 * hw)]
    sub x2 -> x0, matrix products: 7.41 us -> none  [soft_weights(): raised = jnp.exp(masked - highest)]
  transfers between devices with their start and end apart: 8 -> 0, of which waited for: 5 -> 0; matrix products, arithmetic and copies ran while one was open for 3% -> 0% of each run, Pallas kernels for 0% -> 0%
where the time goes in v1:
time: 74.8 us; the launch traced here: 73.6 us
  Pallas kernels  66.1 us (88%)
  local copies, waits for them, and re-layouts  5.39 us (7%)
  other arithmetic  2.04 us (3%)
    pallas_call x1, Pallas kernels, on_device(): pl.pallas_call(functools.partial(kernel, n, nvar), out_shape=jax.ShapeDty...  66.1 us

profile of v1, /device:TPU:0, one launch (start us, length us, event | category | flops | bytes accessed | tf_op | source)
XLA Modules:
  0.0 73.6 jit_solution(8284117818271261049)
XLA Ops:
  0.0 0.7 convert_bitcast_fusion
  0.7 0.7 broadcast_in_dim.10.tgain
  1.4 0.7 broadcast_in_dim.11.sgain
  2.1 0.2 dynamic_update_slice.3.marks
  2.3 1.2 %fusion = (bf16[768,1,192]{0,2,1:T(8,128)(2,1)S(1)}, bf16[768,1,192]{0,2,1:T(8,128)(2,1)S(1)}, bf16[768,1,192]{0,2,1:T(8,128)(2,1)S(1)}) fusion(bf16[768,3,192]{0,2,1:T(8,128)(2,1)} %param.16), kind=kLoop, calls=%fused_computation.2 | loop fusion | bytes 1769472 | tf_op jit(solution)/shard_map/slice | solution.py:290
  3.5 0.2 copy.18
  3.7 0.2 copy.19
  3.9 0.2 copy.20
  4.0 0.0 copy-start.4
  4.1 1.4 %pad_maximum_fusion.wqs_in = bf16[768,576]{1,0:T(8,128)(2,1)} fusion(bf16[768,192]{1,0:T(8,128)(2,1)S(1)} %bitcast.12, bf16[768,192]{1,0:T(8,128)(2,1)S(1)} %bitcast.11, bf16[768,192]{1,0:T(8,128)(2,1)S(1)} %bitcast.10), kind=kLoop, calls=%fused_computation | loop fusion | flops 2654208 | bytes 1769472 | tf_op jit(solution)/shard_map/concatenate | solution.py:290
  5.4 0.0 copy-done.4
  5.4 0.0 copy-start
  5.4 0.0 copy-start.1
  5.4 0.0 copy-start.2
  5.4 0.0 copy-start.3
  5.4 1.3 %copy.17.wt_in = bf16[768,576]{1,0:T(8,128)(2,1)} copy(bf16[768,576]{0,1:T(8,128)(2,1)S(1)} %bitcast.13) | data formatting | bytes 1769472 | tf_op jit(solution)/shard_map/reshape | solution.py:289
  6.8 0.0 copy-done
  6.8 0.0 copy-done.1
  6.8 0.0 copy-done.2
  6.8 0.0 copy-done.3
  6.8 66.1 %shard_map.91 = bf16[3,64,768]{2,1,0:T(8,128)(2,1)S(1)} custom-call(bf16[3,64,768]{2,1,0:T(8,128)(2,1)S(1)} %bitcast.9, f32[8,256]{1,0:T(8,128)S(1)} %dynamic_update_slice.3.marks, s32[24]{0:T(128)S(1)} %copy-done.3, f32[1,768]{1,0:T(1,128)S(1)} %broadcast_in_dim.10.tgain, f32[1,768]{1,0:T(1,128)S(1)} %broadcast_in_dim.11.sgain, ...), custom_call_target="tpu_custom_call" | custom-call | tf_op jit(solution)/shard_map/pallas_call | solution.py:295
  72.9 0.7 copy.23
  (1 shorter events, 0.0 us)
Async XLA Ops:
  4.0 1.4 %copy-start.4 = (bf16[768,3,192]{0,2,1:T(8,128)(2,1)S(1)}, bf16[768,3,192]{0,2,1:T(8,128)(2,1)}, u32[]{:S(2)}) copy-start(bf16[768,3,192]{0,2,1:T(8,128)(2,1)} %param.13) | copy-start | bytes 2654212
  5.4 1.3 %copy-start = (bf16[64,3,768]{2,0,1:T(8,128)(2,1)S(1)}, bf16[64,3,768]{2,0,1:T(8,128)(2,1)}, u32[]{:S(2)}) copy-start(bf16[64,3,768]{2,0,1:T(8,128)(2,1)} %param.9) | copy-start | bytes 884740
  5.4 1.3 %copy-start.1 = (bf16[192,768]{1,0:T(8,128)(2,1)S(1)}, bf16[192,768]{1,0:T(8,128)(2,1)}, u32[]{:S(2)}) copy-start(bf16[192,768]{1,0:T(8,128)(2,1)} %wot_in.1) | copy-start | bytes 884740
  5.4 1.3 %copy-start.2 = (bf16[192,768]{1,0:T(8,128)(2,1)S(1)}, bf16[192,768]{1,0:T(8,128)(2,1)}, u32[]{:S(2)}) copy-start(bf16[192,768]{1,0:T(8,128)(2,1)} %wos_in.1) | copy-start | bytes 884740
  5.4 1.3 %copy-start.3 = (s32[24]{0:T(128)S(1)}, s32[24]{0:T(128)}, u32[]{:S(2)}) copy-start(s32[24]{0:T(128)} %gids.1) | copy-start | bytes 292

commit v2 on v1

v2 whole, which is shorter than its diff:
```python
import functools

import jax
import jax.numpy as jnp
from jax import lax
from jax.experimental import pallas as pl
from jax.experimental.pallas import tpu as pltpu
from jax.sharding import PartitionSpec as P

HD = 64
REACH = 5
EPS = 1e-06
MESH = pl.DeviceIdType.MESH
F32 = jnp.float32
BF16 = jnp.bfloat16


def norm_rows(rows, gain):
    floats = rows.astype(F32)
    scaled = floats * lax.rsqrt(jnp.mean(floats * floats, axis=-1, keepdims=True) + EPS)
    return (scaled * gain).astype(BF16)


def dot(a, b):
    return jnp.dot(a, b, preferred_element_type=F32)


def dot_t(a, b):
    return lax.dot_general(a, b, (((1,), (1,)), ((), ())), preferred_element_type=F32)


def kernel(
    n, nvar, tok, marks, gids, tgain, sgain, wt, wot_in, wqs_in, wos_in,
    out, gx, mk, wot, wqs, wos, att, ratt, mid, sw, kvb, qb, prod, sc, pb,
    local_sem, tok_s, tok_r, mk_s, mk_r, w_s, w_r, att_s, att_r, win_s, win_r,
):
    me = lax.axis_index("patch")
    var = lax.axis_index("var")
    nv, pp, dm = tok.shape
    hw = wot_in.shape[0]
    heads = hw // HD
    side = (me + 1 - 2 * (me % 2), me + 2 - 4 * ((me // 2) % 2), n - 1 - me)
    sib = var + 1 - 2 * (var % 2)
    core = var % 2
    nbrs = (1, -1, 2, -2)

    def exists(k):
        return (var + k >= 0) & (var + k < nvar)

    barrier = pltpu.get_barrier_semaphore()
    count = n - 1 + 1
    for other in side:
        pl.semaphore_signal(barrier, inc=1, device_id={"patch": other}, device_id_type=MESH)
    pl.semaphore_signal(barrier, inc=1, device_id={"var": sib}, device_id_type=MESH)
    for k in nbrs:
        @pl.when(exists(k))
        def _():
            pl.semaphore_signal(barrier, inc=1, device_id={"var": var + k}, device_id_type=MESH)
        count = count + exists(k).astype(jnp.int32)
    own = [
        pltpu.make_async_copy(wot_in, wot.at[me], local_sem.at[0]),
        pltpu.make_async_copy(wqs_in, wqs.at[me], local_sem.at[1]),
        pltpu.make_async_copy(wos_in, wos.at[me], local_sem.at[2]),
    ]
    for c in own:
        c.start()
    pl.semaphore_wait(barrier, count)

    sends = []

    def remote(src, dst, ssem, rsem, **where):
        c = pltpu.make_async_remote_copy(
            src_ref=src, dst_ref=dst, send_sem=ssem, recv_sem=rsem, device_id=where, device_id_type=MESH
        )
        return c

    def launch(*a, **k):
        c = remote(*a, **k)
        c.start()
        sends.append(c)
        return c

    def block(of, lo=0, num=pp):
        return pl.ds(pl.multiple_of(of * pp + lo, num), num)

    half = pp // 2
    mk_c = [launch(marks, mk.at[me], mk_s.at[d], mk_r.at[d], patch=side[d]) for d in range(3)]
    tok_c = {}
    for i in range(nv):
        for d in (0, 1):
            v = i if d == 1 else nv - 1 - i
            tok_c[d, v] = launch(tok.at[v], gx.at[v, block(me), :], tok_s.at[d, v], tok_r.at[d, v], patch=side[d])
    routes = ((1, 0, 0, pp), (0, 2, 0, pp), (1, 1, 0, half), (0, 1, half, half))
    diag_c = []
    for i, (d, v, lo, num) in enumerate(routes):
        tok_c[d, v].wait_recv()
        piece = gx.at[v, block(side[d], lo, num), :]
        diag_c.append(launch(piece, piece, tok_s.at[2, i], tok_r.at[2, i], patch=side[1 - d]))

    arrays = ((wot_in, wot), (wqs_in, wqs), (wos_in, wos))
    wc = {}

    def piece_of(a, shard, part=None):
        rows = arrays[a][1].shape[1] // 2
        if part is None:
            return arrays[a][1].at[shard, pl.ds(pl.multiple_of(core * rows, rows), rows), :]
        num = rows // 2
        return arrays[a][1].at[shard, pl.ds(pl.multiple_of(core * rows + part * num, num), num), :]

    def w_own(a):
        src = arrays[a][0]
        rows = src.shape[0] // 2
        for d in (0, 1):
            wc[a, d] = launch(
                src.at[pl.ds(pl.multiple_of(core * rows, rows), rows), :], piece_of(a, me),
                w_s.at[a, d], w_r.at[a, d], patch=side[d],
            )

    def w_relay(a):
        for d in (0, 1):
            wc[a, d].wait_recv()
            piece = piece_of(a, side[d], 1 - d)
            wc[a, 2 + d] = launch(piece, piece, w_s.at[a, 2 + d], w_r.at[a, 2 + d], patch=side[1 - d])
            piece = piece_of(a, side[d])
            wc[a, 4 + d] = launch(piece, piece, w_s.at[a, 4 + d], w_r.at[a, 4 + d], var=sib)

    def w_diag(a):
        wc[a, 2].wait_recv()
        wc[a, 3].wait_recv()
        piece = piece_of(a, side[2])
        wc[a, 6] = launch(piece, piece, w_s.at[a, 6], w_r.at[a, 6], var=sib)

    w_own(0)
    for k in nbrs:
        lo = {1: 9, -1: 3, 2: 12, -2: 1}[k]
        num = nv if abs(k) == 1 else nv - 1

        @pl.when(jnp.logical_not(exists(k)))
        def _():
            sw[lo:lo + num] = jnp.zeros((num, pp, dm), BF16)

    gx[:, block(me), :] = tok[...]
    mk[me] = marks[...]
    for c in mk_c:
        c.wait_recv()
    for d in (0, 1):
        for v in range(nv):
            if (d, v) not in [r[:2] for r in routes]:
                tok_c[d, v].wait_recv()
    for c in diag_c:
        c.wait_recv()

    full = n * pp
    seen = jnp.concatenate([mk[s] for s in range(n)], axis=1)
    qi = lax.broadcasted_iota(jnp.int32, (full, full), 0)
    ki = lax.broadcasted_iota(jnp.int32, (full, full), 1)
    att_c = []
    for v in range(nv):
        normed = norm_rows(gx[v], tgain[...])
        proj = dot_t(normed, wt[...]).astype(BF16)
        allowed = ((ki < qi) & (seen[v:v + 1, :] > 0)) | (ki == qi)
        outs = []
        for h in range(heads):
            q = proj[:, h * HD:(h + 1) * HD]
            k = proj[:, hw + h * HD:hw + (h + 1) * HD]
            val = proj[:, 2 * hw + h * HD:2 * hw + (h + 1) * HD]
            s = lax.dot_general(q, k, (((1,), (1,)), ((), ())), preferred_element_type=F32) * HD ** (-0.5)
            s = jnp.where(allowed, s, -jnp.inf)
            e = jnp.exp(s - jnp.max(s, axis=-1, keepdims=True))
            w = (e / jnp.sum(e, axis=-1, keepdims=True)).astype(BF16)
            outs.append(dot(w, val).astype(BF16))
        att[v] = jnp.concatenate(outs, axis=1)
        for d in (2, 0, 1):
            att_c.append(launch(att.at[v, block(side[d]), :], ratt.at[me, v], att_s.at[v, d], att_r.at[v, d], patch=side[d]))
        ratt[me, v] = att[v, block(me), :]
    w_relay(0)
    w_own(1)
    own[0].wait()
    for c in att_c:
        c.wait_recv()
    w_diag(0)
    for k in (4, 5, 6):
        wc[0, k].wait_recv()

    rows = nv * pp
    mix = jnp.zeros((rows, dm), F32)
    for s in range(n):
        mix = mix + dot(ratt[s].reshape(rows, hw), wot[s]).astype(BF16).astype(F32)
    middle = (tok[...].reshape(rows, dm).astype(F32) + mix).astype(BF16)
    mid[...] = middle
    sw[6:6 + nv] = norm_rows(middle, sgain[...]).reshape(nv, pp, dm)

    def window(k, i):
        src = {1: (6, 9), -1: (6, 9), 2: (7, 9), -2: (6, 8)}[k]
        dst = {1: (3, 6), -1: (9, 12), 2: (1, 3), -2: (12, 14)}[k]
        return remote(sw.at[src[0]:src[1]], sw.at[dst[0]:dst[1]], win_s.at[i], win_r.at[i], var=var + k)

    for i, k in enumerate(nbrs):
        @pl.when(exists(k))
        def _():
            window(k, i).start()

    own[1].wait()
    own[2].wait()
    for i, k in enumerate(nbrs):
        @pl.when(exists(-k))
        def _():
            window(k, i).wait_recv()

    nkey = 4 + 3 * nv
    pairs = [(u, u + 6 + t) for u in range(nv) for t in range(-REACH, REACH + 1)]
    sc[...] = jnp.zeros_like(sc)

    def scores_of(s):
        qb[...] = dot_t(sw[6:6 + nv].reshape(rows, dm), wqs[s, :hw, :]).astype(BF16).reshape(nv, pp, hw)
        kvb[s] = dot_t(sw[1:1 + nkey].reshape(nkey * pp, dm), wqs[s, hw:, :]).astype(BF16).reshape(nkey, pp, 2 * hw)
        for i, (u, j) in enumerate(pairs):
            prod[i * pp:(i + 1) * pp, :] = (
                qb[u].astype(F32) * kvb[s, j - 1, :, :hw].astype(F32)
            ).astype(BF16)
        lane = lax.broadcasted_iota(jnp.int32, (hw, 128), 0) // HD + heads * s
        col = lax.broadcasted_iota(jnp.int32, (hw, 128), 1)
        sc[...] += dot(prod[...], (lane == col).astype(F32).astype(BF16))

    scores_of(me)
    w_relay(1)
    w_own(2)
    for d in (0, 1):
        wc[1, 4 + d].wait_recv()
        scores_of(side[d])
    w_diag(1)
    wc[1, 6].wait_recv()
    scores_of(side[2])
    w_relay(2)

    total = gids.shape[0]
    local_n = total // nv
    base = (var % local_n) * nv
    for u in range(nv):
        mine_group = gids[base + u]
        slabs = []
        for t in range(-REACH, REACH + 1):
            w = base + u + t
            inside = (w >= 0) & (w < total)
            at = jnp.minimum(jnp.maximum(w, 0), total - 1)
            i = pairs.index((u, u + 6 + t))
            ok = inside & (gids[at] == mine_group)
            slabs.append(jnp.where(ok, sc[i * pp:(i + 1) * pp, :] * HD ** (-0.5), -jnp.inf))
        top = functools.reduce(jnp.maximum, slabs)
        es = [jnp.exp(x - top) for x in slabs]
        den = functools.reduce(lambda a, b: a + b, es)
        for t, e in enumerate(es):
            i = u * (2 * REACH + 1) + t
            pb[i * pp:(i + 1) * pp, :] = (e / den).astype(BF16)

    def mix_of(s):
        lane = lax.broadcasted_iota(jnp.int32, (128, hw), 1) // HD + heads * s
        col = lax.broadcasted_iota(jnp.int32, (128, hw), 0)
        spread = (lane == col).astype(F32).astype(BF16)
        done = []
        for u in range(nv):
            total_u = jnp.zeros((pp, hw), F32)
            lo = u * (2 * REACH + 1)
            wide = dot(pb[lo * pp:(lo + 2 * REACH + 1) * pp, :], spread)
            for t in range(2 * REACH + 1):
                val = kvb[s, u + t, :, hw:].astype(F32)
                total_u = total_u + wide[t * pp:(t + 1) * pp] * val
            done.append(total_u.astype(BF16))
        res = dot(jnp.concatenate(done, axis=0), wos[s]).astype(BF16).astype(F32)
        return res

    mix2 = mix_of(me)
    for d in (0, 1):
        wc[2, 4 + d].wait_recv()
        mix2 = mix2 + mix_of(side[d])
    w_diag(2)
    wc[2, 6].wait_recv()
    mix2 = mix2 + mix_of(side[2])
    out[...] = (mid[...].astype(F32) + mix2).astype(BF16).reshape(nv, pp, dm)

    for c in sends:
        c.wait_send()
    for i, k in enumerate(nbrs):
        @pl.when(exists(k))
        def _():
            window(k, i).wait_send()


def on_device(n, nvar, tokens, patch_mask, group_ids, time_gain, time_qkv, time_out, space_gain, space_qkv, space_out):
    pp, nv, dm = tokens.shape
    hw = time_out.shape[0]
    tok = jnp.transpose(tokens, (1, 0, 2))
    wt = jnp.transpose(time_qkv, (1, 2, 0)).reshape(3 * hw, dm)
    wqs = jnp.transpose(space_qkv, (1, 2, 0)).reshape(3 * hw, dm)
    npair = nv * (2 * REACH + 1)
    vm = pl.BlockSpec(memory_space=pltpu.VMEM)
    anyv = pl.BlockSpec(memory_space=pl.ANY)
    dma = pltpu.SemaphoreType.DMA
    res = pl.pallas_call(
        functools.partial(kernel, n, nvar),
        out_shape=jax.ShapeDtypeStruct((nv, pp, dm), BF16),
        in_specs=[vm, vm, pl.BlockSpec(memory_space=pltpu.SMEM), vm, vm, vm, anyv, anyv, anyv],
        out_specs=vm,
        scratch_shapes=[
            pltpu.VMEM((nv, n * pp, dm), BF16),
            pltpu.VMEM((n, nv, pp), jnp.int32),
            pltpu.VMEM((n, hw, dm), BF16),
            pltpu.VMEM((n, 3 * hw, dm), BF16),
            pltpu.VMEM((n, hw, dm), BF16),
            pltpu.VMEM((nv, n * pp, hw), BF16),
            pltpu.VMEM((n, nv, pp, hw), BF16),
            pltpu.VMEM((nv * pp, dm), BF16),
            pltpu.VMEM((5 * nv, pp, dm), BF16),
            pltpu.VMEM((n, 4 + 3 * nv, pp, 2 * hw), BF16),
            pltpu.VMEM((nv, pp, hw), BF16),
            pltpu.VMEM((npair * pp, hw), BF16),
            pltpu.VMEM((npair * pp, 128), F32),
            pltpu.VMEM((npair * pp, 128), BF16),
            dma((3,)), dma((3, 4)), dma((3, 4)), dma((3,)), dma((3,)),
            dma((3, 7)), dma((3, 7)), dma((nv, 3)), dma((nv, 3)), dma((4,)), dma((4,)),
        ],
        compiler_params=pltpu.CompilerParams(
            collective_id=0, has_side_effects=True, vmem_limit_bytes=52 * 2**20
        ),
    )(tok, patch_mask.T, group_ids, time_gain, space_gain, wt, time_out, wqs, space_out)
    return jnp.transpose(res, (1, 0, 2))


def solution(mesh):
    in_specs = (
        P("patch", ("parts", "var"), None),
        P("patch", ("parts", "var")),
        P("parts"),
        P(),
        P(None, None, "patch"),
        P("patch", None),
        P(),
        P(None, None, "patch"),
        P("patch", None),
    )
    out_specs = P("patch", ("parts", "var"), None)
    return jax.shard_map(
        functools.partial(on_device, mesh.shape["patch"], mesh.shape["var"]),
        mesh=mesh, in_specs=in_specs, out_specs=out_specs, check_vma=False,
    )
```

time: 74.8 us -> 59.8 us (0.80); the launches traced: 73.6 us -> 59.5 us
  Pallas kernels: 66.1 us -> 54.5 us
  other arithmetic: 2.04 us -> 0 us
    pallas_call x1, Pallas kernels: 66.1 us -> 54.5 us  [on_device(): pl.pallas_call(functools.partial(kernel, n, nvar), out_shape=jax.ShapeDty...]
    unnamed x14 -> x15, local copies, waits for them, and re-layouts: 1.25 us -> 4.98 us
    broadcast_in_dim x3 -> x0, local copies, waits for them, and re-layouts: 1.38 us -> none  [the longest x1 0.69 us: on_device(): space_gain[None]]
    concatenate x1 -> x0, other arithmetic: 1.35 us -> none  [on_device(): jnp.concatenate([space_qkv[:, 1], space_qkv[:, 2], space_qkv[:, 0]], axis=1)]
    reshape x1 -> x0, local copies, waits for them, and re-layouts: 1.32 us -> none  [on_device(): wt = time_qkv.reshape(dm, 3 * hw)]
    slice x1 -> x0, local copies, waits for them, and re-layouts: 1.2 us -> none  [on_device(): space_qkv[:, 1]]
where the time goes in v2:
time: 59.8 us; the launch traced here: 59.5 us
  Pallas kernels  54.5 us (91%)
  local copies, waits for them, and re-layouts  4.98 us (8%)
    pallas_call x1, Pallas kernels, on_device(): pl.pallas_call(functools.partial(kernel, n, nvar), out_shape=jax.ShapeDty...  54.5 us
    unnamed x15, local copies, waits for them, and re-layouts  4.98 us

profile of v2, /device:TPU:0, one launch (start us, length us, event | category | flops | bytes accessed | tf_op | source)
XLA Modules:
  0.0 59.5 jit_solution(17126690144548708634)
XLA Ops:
  0.0 0.0 copy-start.3
  0.0 0.0 copy-start.5
  0.0 0.0 copy-start.6
  0.0 0.7 %copy-done.3 = f32[768]{0:T(1024)S(1)} copy-done((f32[768]{0:T(1024)S(1)}, f32[768]{0:T(1024)}, u32[]{:S(2)}) %copy-start.3) | copy-done | bytes 3096
  0.7 0.0 copy-done.5
  0.7 0.0 copy-done.6
  0.7 0.0 copy-start
  0.7 1.0 %copy-done = bf16[64,3,768]{2,0,1:T(8,128)(2,1)S(1)} copy-done((bf16[64,3,768]{2,0,1:T(8,128)(2,1)S(1)}, bf16[64,3,768]{2,0,1:T(8,128)(2,1)}, u32[]{:S(2)}) %copy-start) | copy-done | bytes 294936
  1.7 0.0 copy-start.1
  1.7 1.0 %copy-done.1 = bf16[192,768]{1,0:T(8,128)(2,1)S(1)} copy-done((bf16[192,768]{1,0:T(8,128)(2,1)S(1)}, bf16[192,768]{1,0:T(8,128)(2,1)}, u32[]{:S(2)}) %copy-start.1) | copy-done | bytes 294936
  2.6 0.0 copy-start.2
  2.6 1.0 %copy-done.2 = bf16[192,768]{1,0:T(8,128)(2,1)S(1)} copy-done((bf16[192,768]{1,0:T(8,128)(2,1)S(1)}, bf16[192,768]{1,0:T(8,128)(2,1)}, u32[]{:S(2)}) %copy-start.2) | copy-done | bytes 294936
  3.6 0.0 copy-start.4
  3.6 0.7 %copy-done.4 = f32[768]{0:T(1024)S(1)} copy-done((f32[768]{0:T(1024)S(1)}, f32[768]{0:T(1024)}, u32[]{:S(2)}) %copy-start.4) | copy-done | bytes 3096
  4.3 54.5 %shard_map.91 = bf16[3,64,768]{2,1,0:T(8,128)(2,1)S(1)} custom-call(bf16[3,64,768]{2,1,0:T(8,128)(2,1)S(1)} %bitcast.10, s32[3,64]{1,0:T(4,128)S(1)} %bitcast.11, s32[24]{0:T(128)S(1)} %copy-done.6, f32[768]{0:T(1024)S(1)} %copy-done.3, f32[768]{0:T(1024)S(1)} %copy-done.4, bf16[576,768]{1,0:T(8,128)(2,1)} %bitcast.12, bf16[192,768]{1,0:T(8,128)(2,1)S(1)} %copy-done.1, ...), custom_call_target="tpu_custom_call" | custom-call | tf_op jit(solution)/shard_map/pallas_call | solution.py:299
  58.8 0.7 %copy.11 = bf16[64,3,768]{2,0,1:T(8,128)(2,1)} copy(bf16[64,3,768]{2,0,1:T(8,128)(2,1)S(1)} %bitcast.9) | data formatting | bytes 589824
Async XLA Ops:
  0.0 0.7 %copy-start.3 = (f32[768]{0:T(1024)S(1)}, f32[768]{0:T(1024)}, u32[]{:S(2)}) copy-start(f32[768]{0:T(1024)} %tgain.1) | copy-start | bytes 9220
  0.0 0.7 %copy-start.5 = (s32[64,3]{0,1:T(4,128)S(1)}, s32[64,3]{0,1:T(4,128)}, u32[]{:S(2)}) copy-start(s32[64,3]{0,1:T(4,128)} %param.10) | copy-start | bytes 2308
  0.0 0.7 %copy-start.6 = (s32[24]{0:T(128)S(1)}, s32[24]{0:T(128)}, u32[]{:S(2)}) copy-start(s32[24]{0:T(128)} %gids.1) | copy-start | bytes 292
  0.7 1.0 %copy-start = (bf16[64,3,768]{2,0,1:T(8,128)(2,1)S(1)}, bf16[64,3,768]{2,0,1:T(8,128)(2,1)}, u32[]{:S(2)}) copy-start(bf16[64,3,768]{2,0,1:T(8,128)(2,1)} %param.9) | copy-start | bytes 884740
  1.7 1.0 %copy-start.1 = (bf16[192,768]{1,0:T(8,128)(2,1)S(1)}, bf16[192,768]{1,0:T(8,128)(2,1)}, u32[]{:S(2)}) copy-start(bf16[192,768]{1,0:T(8,128)(2,1)} %wot_in.1) | copy-start | bytes 884740
  2.6 1.0 %copy-start.2 = (bf16[192,768]{1,0:T(8,128)(2,1)S(1)}, bf16[192,768]{1,0:T(8,128)(2,1)}, u32[]{:S(2)}) copy-start(bf16[192,768]{1,0:T(8,128)(2,1)} %wos_in.1) | copy-start | bytes 884740
  3.6 0.7 %copy-start.4 = (f32[768]{0:T(1024)S(1)}, f32[768]{0:T(1024)}, u32[]{:S(2)}) copy-start(f32[768]{0:T(1024)} %sgain.1) | copy-start | bytes 9220

commit v3 on v2

--- a/solution.py
+++ b/solution.py
@@ -30,8 +30,8 @@
 
 
 def kernel(
-    n, nvar, tok, marks, gids, tgain, sgain, wt, wot_in, wqs_in, wos_in,
-    out, gx, mk, wot, wqs, wos, att, ratt, mid, sw, kvb, qb, prod, sc, pb,
+    n, nvar, tok, marks, gids, tgain, sgain, wt_in, wot_in, wqs_in, wos_in,
+    out, gx, mk, wt, wot, wqs, wos, att, ratt, mid, sw, kvb, qb, prod, sc, pb,
     local_sem, tok_s, tok_r, mk_s, mk_r, w_s, w_r, att_s, att_r, win_s, win_r,
 ):
     me = lax.axis_index("patch")
@@ -61,9 +61,11 @@
         pltpu.make_async_copy(wot_in, wot.at[me], local_sem.at[0]),
         pltpu.make_async_copy(wqs_in, wqs.at[me], local_sem.at[1]),
         pltpu.make_async_copy(wos_in, wos.at[me], local_sem.at[2]),
+        pltpu.make_async_copy(wt_in, wt, local_sem.at[3]),
+        pltpu.make_async_copy(tok, gx.at[:, pl.ds(pl.multiple_of(me * pp, pp), pp), :], local_sem.at[4]),
     ]
-    for c in own:
-        c.start()
+    for i in (4, 3, 0, 1, 2):
+        own[i].start()
     pl.semaphore_wait(barrier, count)
 
     sends = []
@@ -139,8 +141,9 @@
         def _():
             sw[lo:lo + num] = jnp.zeros((num, pp, dm), BF16)
 
-    gx[:, block(me), :] = tok[...]
     mk[me] = marks[...]
+    own[3].wait()
+    own[4].wait()
     for c in mk_c:
         c.wait_recv()
     for d in (0, 1):
@@ -186,7 +189,7 @@
     mix = jnp.zeros((rows, dm), F32)
     for s in range(n):
         mix = mix + dot(ratt[s].reshape(rows, hw), wot[s]).astype(BF16).astype(F32)
-    middle = (tok[...].reshape(rows, dm).astype(F32) + mix).astype(BF16)
+    middle = (gx[:, block(me), :].reshape(rows, dm).astype(F32) + mix).astype(BF16)
     mid[...] = middle
     sw[6:6 + nv] = norm_rows(middle, sgain[...]).reshape(nv, pp, dm)
 
@@ -200,8 +203,10 @@
         def _():
             window(k, i).start()
 
+    w_own(2)
     own[1].wait()
     own[2].wait()
+    w_relay(1)
     for i, k in enumerate(nbrs):
         @pl.when(exists(-k))
         def _():
@@ -222,36 +227,26 @@
         col = lax.broadcasted_iota(jnp.int32, (hw, 128), 1)
         sc[...] += dot(prod[...], (lane == col).astype(F32).astype(BF16))
 
-    scores_of(me)
-    w_relay(1)
-    w_own(2)
-    for d in (0, 1):
-        wc[1, 4 + d].wait_recv()
-        scores_of(side[d])
-    w_diag(1)
-    wc[1, 6].wait_recv()
-    scores_of(side[2])
-    w_relay(2)
-
-    total = gids.shape[0]
-    local_n = total // nv
-    base = (var % local_n) * nv
-    for u in range(nv):
-        mine_group = gids[base + u]
-        slabs = []
-        for t in range(-REACH, REACH + 1):
-            w = base + u + t
-            inside = (w >= 0) & (w < total)
-            at = jnp.minimum(jnp.maximum(w, 0), total - 1)
-            i = pairs.index((u, u + 6 + t))
-            ok = inside & (gids[at] == mine_group)
-            slabs.append(jnp.where(ok, sc[i * pp:(i + 1) * pp, :] * HD ** (-0.5), -jnp.inf))
-        top = functools.reduce(jnp.maximum, slabs)
-        es = [jnp.exp(x - top) for x in slabs]
-        den = functools.reduce(lambda a, b: a + b, es)
-        for t, e in enumerate(es):
-            i = u * (2 * REACH + 1) + t
-            pb[i * pp:(i + 1) * pp, :] = (e / den).astype(BF16)
+    def soften():
+        total = gids.shape[0]
+        local_n = total // nv
+        base = (var % local_n) * nv
+        for u in range(nv):
+            mine_group = gids[base + u]
+            slabs = []
+            for t in range(-REACH, REACH + 1):
+                w = base + u + t
+                inside = (w >= 0) & (w < total)
+                at = jnp.minimum(jnp.maximum(w, 0), total - 1)
+                i = pairs.index((u, u + 6 + t))
+                ok = inside & (gids[at] == mine_group)
+                slabs.append(jnp.where(ok, sc[i * pp:(i + 1) * pp, :] * HD ** (-0.5), -jnp.inf))
+            top = functools.reduce(jnp.maximum, slabs)
+            es = [jnp.exp(x - top) for x in slabs]
+            den = functools.reduce(lambda a, b: a + b, es)
+            for t, e in enumerate(es):
+                i = u * (2 * REACH + 1) + t
+                pb[i * pp:(i + 1) * pp, :] = (e / den).astype(BF16)
 
     def mix_of(s):
         lane = lax.broadcasted_iota(jnp.int32, (128, hw), 1) // HD + heads * s
@@ -269,11 +264,21 @@
         res = dot(jnp.concatenate(done, axis=0), wos[s]).astype(BF16).astype(F32)
         return res
 
+    scores_of(me)
+    for d in (0, 1):
+        wc[1, 4 + d].wait_recv()
+        scores_of(side[d])
+    soften()
     mix2 = mix_of(me)
+    w_relay(2)
     for d in (0, 1):
         wc[2, 4 + d].wait_recv()
         mix2 = mix2 + mix_of(side[d])
+    w_diag(1)
     w_diag(2)
+    wc[1, 6].wait_recv()
+    scores_of(side[2])
+    soften()
     wc[2, 6].wait_recv()
     mix2 = mix2 + mix_of(side[2])
     out[...] = (mid[...].astype(F32) + mix2).astype(BF16).reshape(nv, pp, dm)
@@ -294,16 +299,17 @@
     wqs = jnp.transpose(space_qkv, (1, 2, 0)).reshape(3 * hw, dm)
     npair = nv * (2 * REACH + 1)
     vm = pl.BlockSpec(memory_space=pltpu.VMEM)
-    anyv = pl.BlockSpec(memory_space=pl.ANY)
+    anyv = pl.BlockSpec(memory_space=pltpu.HBM)
     dma = pltpu.SemaphoreType.DMA
     res = pl.pallas_call(
         functools.partial(kernel, n, nvar),
         out_shape=jax.ShapeDtypeStruct((nv, pp, dm), BF16),
-        in_specs=[vm, vm, pl.BlockSpec(memory_space=pltpu.SMEM), vm, vm, vm, anyv, anyv, anyv],
+        in_specs=[anyv, vm, pl.BlockSpec(memory_space=pltpu.SMEM), vm, vm, anyv, anyv, anyv, anyv],
         out_specs=vm,
         scratch_shapes=[
             pltpu.VMEM((nv, n * pp, dm), BF16),
             pltpu.VMEM((n, nv, pp), jnp.int32),
+            pltpu.VMEM((3 * hw, dm), BF16),
             pltpu.VMEM((n, hw, dm), BF16),
             pltpu.VMEM((n, 3 * hw, dm), BF16),
             pltpu.VMEM((n, hw, dm), BF16),
@@ -316,11 +322,11 @@
             pltpu.VMEM((npair * pp, hw), BF16),
             pltpu.VMEM((npair * pp, 128), F32),
             pltpu.VMEM((npair * pp, 128), BF16),
-            dma((3,)), dma((3, 4)), dma((3, 4)), dma((3,)), dma((3,)),
+            dma((5,)), dma((3, 4)), dma((3, 4)), dma((3,)), dma((3,)),
             dma((3, 7)), dma((3, 7)), dma((nv, 3)), dma((nv, 3)), dma((4,)), dma((4,)),
         ],
         compiler_params=pltpu.CompilerParams(
-            collective_id=0, has_side_effects=True, vmem_limit_bytes=52 * 2**20
+            collective_id=0, has_side_effects=True, vmem_limit_bytes=67_000_000
         ),
     )(tok, patch_mask.T, group_ids, time_gain, space_gain, wt, time_out, wqs, space_out)
     return jnp.transpose(res, (1, 0, 2))

time: 59.8 us -> 53.9 us (0.901)
  local copies, waits for them, and re-layouts: 4.98 us -> 1.69 us
  Pallas kernels: 54.5 us -> 52.1 us
    unnamed x15 -> x1, local copies, waits for them, and re-layouts: 4.98 us -> 1.69 us
    pallas_call x1, Pallas kernels: 54.5 us -> 52.1 us  [on_device(): pl.pallas_call(functools.partial(kernel, n, nvar), out_shape=jax.ShapeDty...]
where the time goes in v3:
time: 53.9 us; the launch traced here: 53.8 us
  Pallas kernels  52.1 us (97%)
  local copies, waits for them, and re-layouts  1.69 us (3%)
    pallas_call x1, Pallas kernels, on_device(): pl.pallas_call(functools.partial(kernel, n, nvar), out_shape=jax.ShapeDty...  52.1 us
    unnamed x1, local copies, waits for them, and re-layouts  1.69 us

profile of v3, /device:TPU:0, one launch (start us, length us, event | category | flops | bytes accessed | tf_op | source)
XLA Modules:
  0.0 53.8 jit_solution(11740628795906284767)
XLA Ops:
  0.0 52.1 %shard_map.91 = bf16[3,64,768]{2,1,0:T(8,128)(2,1)} custom-call(bf16[3,64,768]{2,1,0:T(8,128)(2,1)} %bitcast.12, s32[3,64]{1,0:T(4,128)} %bitcast.13, s32[24]{0:T(128)} %gids.1, f32[768]{0:T(1024)} %tgain.1, f32[768]{0:T(1024)} %sgain.1, bf16[576,768]{1,0:T(8,128)(2,1)} %bitcast.10, bf16[192,768]{1,0:T(8,128)(2,1)} %wot_in.1, bf16[576,768]{1,0:T(8,128)(2,1)} %bitcast.11, ...), custom_call_target="tpu_custom_call" | custom-call | tf_op jit(solution)/shard_map/pallas_call | solution.py:304
  52.1 1.7 %copy.11 = bf16[64,3,768]{2,0,1:T(8,128)(2,1)} copy(bf16[64,3,768]{2,0,1:T(8,128)(2,1)} %bitcast.9) | data formatting | bytes 589824

commit v4 on v3

--- a/solution.py
+++ b/solution.py
@@ -133,6 +133,7 @@
         wc[a, 6] = launch(piece, piece, w_s.at[a, 6], w_r.at[a, 6], var=sib)
 
     w_own(0)
+    w_own(2)
     for k in nbrs:
         lo = {1: 9, -1: 3, 2: 12, -2: 1}[k]
         num = nv if abs(k) == 1 else nv - 1
@@ -203,10 +204,10 @@
         def _():
             window(k, i).start()
 
-    w_own(2)
     own[1].wait()
     own[2].wait()
     w_relay(1)
+    w_relay(2)
     for i, k in enumerate(nbrs):
         @pl.when(exists(-k))
         def _():
@@ -270,7 +271,6 @@
         scores_of(side[d])
     soften()
     mix2 = mix_of(me)
-    w_relay(2)
     for d in (0, 1):
         wc[2, 4 + d].wait_recv()
         mix2 = mix2 + mix_of(side[d])

time: 53.9 us -> 54 us (level)
  the two profiles are of different devices: /device:TPU:0 before, /device:TPU:1 now
where the time goes in v4:
time: 54 us; the launch traced here: 53.9 us
  Pallas kernels  52.2 us (97%)
  local copies, waits for them, and re-layouts  1.69 us (3%)
    pallas_call x1, Pallas kernels, on_device(): pl.pallas_call(functools.partial(kernel, n, nvar), out_shape=jax.ShapeDty...  52.2 us
    unnamed x1, local copies, waits for them, and re-layouts  1.69 us

profile of v4, /device:TPU:1, one launch (start us, length us, event | category | flops | bytes accessed | tf_op | source)
XLA Modules:
  0.0 53.9 jit_solution(1437260769664466784)
XLA Ops:
  0.0 52.2 %shard_map.91 = bf16[3,64,768]{2,1,0:T(8,128)(2,1)} custom-call(bf16[3,64,768]{2,1,0:T(8,128)(2,1)} %bitcast.12, s32[3,64]{1,0:T(4,128)} %bitcast.13, s32[24]{0:T(128)} %gids.1, f32[768]{0:T(1024)} %tgain.1, f32[768]{0:T(1024)} %sgain.1, bf16[576,768]{1,0:T(8,128)(2,1)} %bitcast.10, bf16[192,768]{1,0:T(8,128)(2,1)} %wot_in.1, bf16[576,768]{1,0:T(8,128)(2,1)} %bitcast.11, ...), custom_call_target="tpu_custom_call" | custom-call | tf_op jit(solution)/shard_map/pallas_call | solution.py:304
  52.2 1.7 %copy.11 = bf16[64,3,768]{2,0,1:T(8,128)(2,1)} copy(bf16[64,3,768]{2,0,1:T(8,128)(2,1)} %bitcast.9) | data formatting | bytes 589824

commit v5 on v4

--- a/solution.py
+++ b/solution.py
@@ -269,12 +269,12 @@
     for d in (0, 1):
         wc[1, 4 + d].wait_recv()
         scores_of(side[d])
+    w_diag(1)
     soften()
     mix2 = mix_of(me)
     for d in (0, 1):
         wc[2, 4 + d].wait_recv()
         mix2 = mix2 + mix_of(side[d])
-    w_diag(1)
     w_diag(2)
     wc[1, 6].wait_recv()
     scores_of(side[2])

time: 54 us -> 53.8 us (level)
  the two profiles are of different devices: /device:TPU:1 before, /device:TPU:0 now
where the time goes in v5:
time: 53.8 us; the launch traced here: 53.6 us
  Pallas kernels  51.9 us (96%)
  local copies, waits for them, and re-layouts  1.69 us (3%)
    pallas_call x1, Pallas kernels, on_device(): pl.pallas_call(functools.partial(kernel, n, nvar), out_shape=jax.ShapeDty...  51.9 us
    unnamed x1, local copies, waits for them, and re-layouts  1.69 us

profile of v5, /device:TPU:0, one launch (start us, length us, event | category | flops | bytes accessed | tf_op | source)
XLA Modules:
  0.0 53.6 jit_solution(8685583336643167317)
XLA Ops:
  0.0 51.9 %shard_map.91 = bf16[3,64,768]{2,1,0:T(8,128)(2,1)} custom-call(bf16[3,64,768]{2,1,0:T(8,128)(2,1)} %bitcast.12, s32[3,64]{1,0:T(4,128)} %bitcast.13, s32[24]{0:T(128)} %gids.1, f32[768]{0:T(1024)} %tgain.1, f32[768]{0:T(1024)} %sgain.1, bf16[576,768]{1,0:T(8,128)(2,1)} %bitcast.10, bf16[192,768]{1,0:T(8,128)(2,1)} %wot_in.1, bf16[576,768]{1,0:T(8,128)(2,1)} %bitcast.11, ...), custom_call_target="tpu_custom_call" | custom-call | tf_op jit(solution)/shard_map/pallas_call | solution.py:304
  51.9 1.7 %copy.11 = bf16[64,3,768]{2,0,1:T(8,128)(2,1)} copy(bf16[64,3,768]{2,0,1:T(8,128)(2,1)} %bitcast.9) | data formatting | bytes 589824
